TPU v7x, 32 devices: a 4x4x1 block of a 4x4x8 slice. The times are simulated.
32 devices in a mesh: dp: 1 (over z), row: 4 (over y), col: 8 (over x, core).
Axes of the slice: x: 4, y: 4, z: 1, core: 2. Of those that a mesh axis runs over, the one named last changes fastest.
The devices are a block of a 4x4x8 slice.
Arguments:
- pair_rep: bfloat16 [768, 768, 128], P(('dp', 'row'), 'col')
- res_mask: int32 [768], P('dp')
- ln_gamma: float32 [128], replicated
- ln_beta: float32 [128], replicated
- w_q: bfloat16 [128, 128], replicated
- w_k: bfloat16 [128, 128], replicated
- w_v: bfloat16 [128, 128], replicated
- w_b: bfloat16 [128, 4], replicated
- w_g: bfloat16 [128, 128], replicated
- w_o: bfloat16 [128, 128], replicated
Outputs:
- output: bfloat16 [768, 768, 128], P(('dp', 'row'), 'col')
All inputs are finite; a program needn't handle non-finite values.
Results may differ from a plain program's by a relative error of at most 0.00711597.
Values are sent between devices in bfloat16 or wider.
A program may use at most 768 MiB of HBM per device.

v0:
```python
import functools

import jax
import jax.numpy as jnp
from jax import lax
from jax.experimental import pallas as pl
from jax.experimental.pallas import tpu as pltpu
from jax.sharding import PartitionSpec as P


LN_EPS = 1e-5
MASKED = -1e9
SAFE = 1e-15
MESH = pl.DeviceIdType.MESH
GROUP = 32
QTILE = 256
KEYBLK = 128
EARLY = 2
VMEM_ALL = 67043328
PAIR = 2
UNROLL = 4
SHARES = (2, 1)


def exchange_kernel(n_col, n_row, z_hbm, gamma_ref, beta_ref, wrep_ref,
                    rows_ref, ball_ref, zv, av, bt, wexp_ref, load_sem, asend, arecv, bsend, brecv, own_sem):
    me = lax.axis_index('col')
    row = lax.axis_index('row')
    parts, rows, width, chan = zv.shape
    n_chip = n_col // 2
    partner = me + 1 - 2 * lax.rem(me, 2)

    loads = []
    order = [2, n_col - 2, n_col // 2]
    order += [k for k in range(1, n_col) if k not in order] + [0]
    dests = [lax.rem(me + k, n_col) for k in order]
    for slot, dest in enumerate(dests):
        load = pltpu.make_async_copy(z_hbm.at[dest], zv.at[slot], load_sem.at[slot])
        load.start()
        loads.append(load)

    barrier = pltpu.get_barrier_semaphore()
    for k in range(1, n_col):
        pl.semaphore_signal(barrier, inc=1, device_id={'col': lax.rem(me + k, n_col)}, device_id_type=MESH)
    for k in range(1, n_row):
        pl.semaphore_signal(barrier, inc=1, device_id={'row': lax.rem(row + k, n_row)}, device_id_type=MESH)
    pl.semaphore_wait(barrier, n_col + n_row - 2)

    stat = jnp.full((2 * chan, chan), 1.0 / chan, jnp.bfloat16)
    gamma = gamma_ref[...]
    beta = beta_ref[...]
    step_rows = rows // 2

    def norm_part(slot, dest):
        def body(step, carry):
            base = step * step_rows
            z_bf = zv[slot, pl.ds(base, step_rows)].reshape(step_rows * width, chan)
            mean = jnp.dot(z_bf, stat[:chan], preferred_element_type=jnp.float32)
            cent = z_bf.astype(jnp.float32) - mean
            sq = cent * cent
            hi = sq.astype(jnp.bfloat16)
            lo = (sq - hi.astype(jnp.float32)).astype(jnp.bfloat16)
            var = jnp.dot(jnp.concatenate([hi, lo], axis=-1), stat, preferred_element_type=jnp.float32)
            normed = cent * lax.rsqrt(var + LN_EPS) * gamma + beta
            av[dest, pl.ds(base, step_rows)] = normed.astype(jnp.bfloat16).reshape(step_rows, width, chan)
            return carry

        lax.fori_loop(0, rows // step_rows, body, 0)

    def row_copy(slot):
        dest = dests[slot]
        return pltpu.make_async_remote_copy(
            av.at[dest], rows_ref.at[me], asend.at[slot], arecv.at[slot],
            device_id={'col': dest}, device_id_type=MESH)

    early = EARLY
    for slot, dest in enumerate(dests):
        loads[slot].wait()
        norm_part(slot, dest)
        if slot < early:
            row_copy(slot).start()
    own = pltpu.make_async_copy(av.at[me], rows_ref.at[me], own_sem.at[0])
    own.start()

    lane = lax.broadcasted_iota(jnp.int32, wrep_ref.shape, 1)
    for jj in range(GROUP):
        wexp_ref[jj * chan:(jj + 1) * chan] = jnp.where(lax.rem(lane, GROUP) == jj, wrep_ref[...], 0.0).astype(jnp.bfloat16)
    tile_rows = parts * rows
    heads = bt.shape[0]
    for grp in range(tile_rows // GROUP):
        flat = [av[(grp * GROUP + jj) // rows, (grp * GROUP + jj) % rows] for jj in range(GROUP)]
        res = jnp.dot(jnp.concatenate(flat, axis=-1), wexp_ref[...], preferred_element_type=jnp.float32)
        for h in range(heads):
            bt[h, :, grp * GROUP:(grp + 1) * GROUP] = res[:, h * GROUP:(h + 1) * GROUP].astype(jnp.bfloat16)

    own_b = pltpu.make_async_copy(bt, ball_ref.at[row, me], own_sem.at[1])
    own_b.start()

    def b_copy(src, src_row, src_col, kind, device):
        return pltpu.make_async_remote_copy(
            src, ball_ref.at[src_row, src_col], bsend.at[kind], brecv.at[kind],
            device_id=device, device_id_type=MESH)

    x_slot = lambda m: m - 1
    y_slot = lambda s, m: (n_chip - 1) + (s - 1) * n_chip + m
    p_slot = lambda s, m: (n_chip - 1) + (n_row - 1) * n_chip + s * n_chip + m
    sent = []
    for m in range(1, n_chip):
        cp = b_copy(bt, row, me, x_slot(m), {'col': lax.rem(me + 2 * m, n_col)})
        cp.start()
        sent.append(cp)
    for s in range(1, n_row):
        cp = b_copy(bt, row, me, y_slot(s, 0), {'row': lax.rem(row + s, n_row)})
        cp.start()
        sent.append(cp)
    cp = b_copy(bt, row, me, p_slot(0, 0), {'col': partner})
    cp.start()
    sent.append(cp)
    for slot in range(early, n_col - 1):
        row_copy(slot).start()

    def block_at(s, m):
        src_row = lax.rem(row + n_row - s, n_row)
        src_col = lax.rem(me + n_col - 2 * m, n_col)
        return src_row, src_col

    for m in range(1, n_chip):
        src_row, src_col = block_at(0, m)
        block = ball_ref.at[src_row, src_col]
        pltpu.make_async_remote_copy(block, block, bsend.at[x_slot(m)], brecv.at[x_slot(m)],
                                     device_id={'col': partner}, device_id_type=MESH).wait_recv()
        for s in range(1, n_row):
            cp = b_copy(block, src_row, src_col, y_slot(s, m), {'row': lax.rem(row + s, n_row)})
            cp.start()
            sent.append(cp)
        cp = b_copy(block, src_row, src_col, p_slot(0, m), {'col': partner})
        cp.start()
        sent.append(cp)
    for m in range(n_chip):
        for s in range(1, n_row):
            src_row, src_col = block_at(s, m)
            block = ball_ref.at[src_row, src_col]
            pltpu.make_async_remote_copy(block, block, bsend.at[y_slot(s, m)], brecv.at[y_slot(s, m)],
                                         device_id={'col': partner}, device_id_type=MESH).wait_recv()
            cp = b_copy(block, src_row, src_col, p_slot(s, m), {'col': partner})
            cp.start()
            sent.append(cp)
    for m in range(n_chip):
        for s in range(n_row):
            src_row = lax.rem(row + n_row - s, n_row)
            src_col = lax.rem(partner + n_col - 2 * m, n_col)
            block = ball_ref.at[src_row, src_col]
            pltpu.make_async_remote_copy(block, block, bsend.at[p_slot(s, m)], brecv.at[p_slot(s, m)],
                                         device_id={'col': partner}, device_id_type=MESH).wait_recv()
    for cp in sent:
        cp.wait_send()
    own_b.wait()
    own.wait()
    for slot in range(n_col - 1):
        row_copy(slot).wait()


def exchange(n_col, n_row, pair_tile, gamma, beta, w_rep, heads):
    row_len, width, chan = pair_tile.shape
    rows = row_len // n_col
    n_bsem = (n_col // 2 - 1) + (n_row - 1) * (n_col // 2) + n_row * (n_col // 2)
    hbm = pl.BlockSpec(memory_space=pl.ANY)
    vmem = pl.BlockSpec(memory_space=pltpu.VMEM)
    return pl.pallas_call(
        functools.partial(exchange_kernel, n_col, n_row),
        name='exchange_rows',
        out_shape=(jax.ShapeDtypeStruct((n_col, rows, width, chan), jnp.bfloat16),
                   jax.ShapeDtypeStruct((n_row, n_col, heads, width, row_len), jnp.bfloat16)),
        in_specs=[hbm, vmem, vmem, vmem],
        out_specs=(hbm, hbm),
        scratch_shapes=[
            pltpu.VMEM((n_col, rows, width, chan), jnp.bfloat16),
            pltpu.VMEM((n_col, rows, width, chan), jnp.bfloat16),
            pltpu.VMEM((heads, width, row_len), jnp.bfloat16),
            pltpu.VMEM((GROUP * chan, heads * GROUP), jnp.bfloat16),
            pltpu.SemaphoreType.DMA((n_col,)),
            pltpu.SemaphoreType.DMA((n_col,)),
            pltpu.SemaphoreType.DMA((n_col,)),
            pltpu.SemaphoreType.DMA((n_bsem,)),
            pltpu.SemaphoreType.DMA((n_bsem,)),
            pltpu.SemaphoreType.DMA((2,)),
        ],
        compiler_params=pltpu.CompilerParams(collective_id=1, has_side_effects=True, vmem_limit_bytes=VMEM_ALL),
    )(pair_tile.reshape(n_col, rows, width, chan), gamma, beta, w_rep)


def attend_kernel(scale, a_ref, ball_ref, mask_ref, wq_ref, wk_ref, wv_ref, wg_ref, out_ref,
                  wqvg_ref, bias, kbuf, qz, vt, gt, og, edge, mcol):
    n_row, n_col, heads, width, row_len = ball_ref.shape
    keys = n_col * width
    chan = a_ref.shape[-1]
    head_dim = chan // heads

    @pl.when(pl.program_id(0) == 0)
    def _():
        qz[...] = jnp.zeros_like(qz)
        for n, w_ref in enumerate((wq_ref, wv_ref, wg_ref)):
            wqvg_ref[n * chan:(n + 1) * chan] = w_ref[...].astype(jnp.float32).T.astype(jnp.bfloat16)
        added = jnp.where(mask_ref[...] > 0, 0.0, MASKED).astype(jnp.float32)
        mcol[...] = jnp.broadcast_to(added, (chan, keys)).T

        def fill(c, carry):
            krange = pl.ds(pl.multiple_of(c * width, width), width)
            mask = mcol[krange, :1]
            for h in range(heads):
                for r in range(n_row):
                    bias[h, krange, r * row_len:(r + 1) * row_len] = ball_ref[r, c, h].astype(jnp.float32) + mask
            return carry

        lax.fori_loop(0, n_col, fill, 0)

    pair = a_ref.shape[1]
    for r in range(pair):
        a = a_ref[:, r].reshape(keys, chan)
        kbuf[r] = jnp.dot(a, wk_ref[...], preferred_element_type=jnp.float32).astype(jnp.bfloat16)
        qvg = lax.dot_general(wqvg_ref[...], a, (((1,), (1,)), ((), ())), preferred_element_type=jnp.float32)
        q_t = (qvg[:chan] * scale).astype(jnp.bfloat16)
        v_t = qvg[chan:2 * chan].astype(jnp.bfloat16)
        gt[r] = jax.nn.sigmoid(qvg[2 * chan:]).reshape(heads, head_dim, keys)
        for h in range(heads):
            qz[r, h, h * head_dim:(h + 1) * head_dim, :] = q_t[h * head_dim:(h + 1) * head_dim]
            vt[r, h] = v_t[h * head_dim:(h + 1) * head_dim]

    def attend(nk):
        def heads_of(step, worst):
            low, high = worst
            r = step // (heads // UNROLL)
            for u in range(UNROLL):
                h = lax.rem(step, heads // UNROLL) * UNROLL + u
                for qt in range(keys // QTILE):
                    cols = slice(qt * QTILE, (qt + 1) * QTILE)
                    q_h = qz[r, h, :, cols]
                    total = None
                    parts = []
                    for kb in range(nk // KEYBLK):
                        kr = slice(kb * KEYBLK, (kb + 1) * KEYBLK)
                        s = jnp.dot(kbuf[r, kr], q_h, preferred_element_type=jnp.float32) + bias[h, kr, cols]
                        p = jnp.exp(s)
                        fold = jnp.sum(p.reshape(KEYBLK // 8, 8, QTILE), axis=0)
                        total = fold if total is None else total + fold
                        parts.append(p.astype(jnp.bfloat16))
                    l = jnp.sum(total, axis=0, keepdims=True)
                    o = jnp.dot(vt[r, h, :, :nk], jnp.concatenate(parts, axis=0), preferred_element_type=jnp.float32)
                    og[r, h, :, cols] = gt[r, h, :, cols] * (o / l)
                    low = jnp.minimum(low, l)
                    high = jnp.maximum(high, jnp.maximum(l, jnp.max(jnp.abs(o), axis=0, keepdims=True)))
            return low, high

        low, high = lax.fori_loop(0, pair * heads // UNROLL, heads_of, (jnp.full((1, QTILE), 1.0, jnp.float32),) * 2)
        edge[0:1] = low
        edge[1:2] = 1.0 / high

    def attend_exact(nk):
        def head(step, carry):
            r, h = step // heads, lax.rem(step, heads)
            for qt in range(keys // QTILE):
                cols = slice(qt * QTILE, (qt + 1) * QTILE)
                s = jnp.dot(kbuf[r, :nk], qz[r, h, :, cols], preferred_element_type=jnp.float32) + bias[h, :nk, cols]
                m = jnp.max(s, axis=0, keepdims=True)
                p = jnp.exp(s - m)
                l = jnp.sum(p, axis=0, keepdims=True)
                o = jnp.dot(vt[r, h, :, :nk], p.astype(jnp.bfloat16), preferred_element_type=jnp.float32)
                og[r, h, :, cols] = gt[r, h, :, cols] * (o / l)
            return carry

        lax.fori_loop(0, pair * heads, head, 0)

    attend(keys)

    @pl.when(jnp.logical_not(jnp.min(edge[...]) > SAFE))
    def _():
        attend_exact(keys)

    for r in range(pair):
        gated = og[r].reshape(chan, keys).T
        out_ref[:, r] = gated.astype(jnp.bfloat16).reshape(n_col, width, chan)


def attend(first, count, a_rows, ball, mask, weights, scale):
    n_col, _, width, chan = a_rows.shape
    _, _, heads, _, _ = ball.shape
    keys = n_col * width
    head_dim = chan // heads
    const = lambda shape: pl.BlockSpec(shape, lambda g: (0,) * len(shape), pipeline_mode=pl.Buffered(1))
    grid_spec = pltpu.PrefetchScalarGridSpec(
        num_scalar_prefetch=0,
        grid=(count // PAIR,),
        in_specs=[
            pl.BlockSpec((n_col, PAIR, width, chan), lambda g: (0, first // PAIR + g, 0, 0)),
            const(ball.shape), const(mask.shape), *[const(w.shape) for w in weights],
        ],
        out_specs=pl.BlockSpec((n_col, PAIR, width, chan), lambda g: (0, g, 0, 0)),
        scratch_shapes=[
            pltpu.VMEM((3 * chan, chan), jnp.bfloat16),
            pltpu.VMEM((heads, keys, keys), jnp.float32),
            pltpu.VMEM((PAIR, keys, chan), jnp.bfloat16),
            pltpu.VMEM((PAIR, heads, chan, keys), jnp.bfloat16),
            pltpu.VMEM((PAIR, heads, head_dim, keys), jnp.bfloat16),
            pltpu.VMEM((PAIR, heads, head_dim, keys), jnp.float32),
            pltpu.VMEM((PAIR, heads, head_dim, keys), jnp.float32),
            pltpu.VMEM((2, QTILE), jnp.float32),
            pltpu.VMEM((keys, chan), jnp.float32),
        ])
    flops = count * (4 * keys * keys * chan * 2 + 8 * keys * chan * chan)
    return pl.pallas_call(
        functools.partial(attend_kernel, scale),
        name='attend_rows',
        grid_spec=grid_spec,
        out_shape=jax.ShapeDtypeStruct((n_col, count, width, chan), jnp.bfloat16),
        cost_estimate=pl.CostEstimate(flops=flops * 20, bytes_accessed=ball.size * 2 + count * keys * chan * 4,
                                      transcendentals=count * heads * keys * keys),
        compiler_params=pltpu.CompilerParams(dimension_semantics=('arbitrary',), vmem_limit_bytes=VMEM_ALL),
    )(a_rows, ball, mask, *weights)


def finish_kernel(z_ref, g_ref, wo_ref, *rest):
    out_ref = rest[-1]
    parts, count, width, chan = z_ref.shape
    for d in range(parts):
        upd = jnp.dot(g_ref[d].reshape(count * width, chan), wo_ref[...], preferred_element_type=jnp.float32)
        z = z_ref[d].reshape(count * width, chan).astype(jnp.float32)
        out_ref[d] = (z + upd).astype(jnp.bfloat16).reshape(count, width, chan)


def finish(first, count, z_parts, gated, w_o, prev):
    n_col, _, width, chan = z_parts.shape
    parts = n_col // 2
    unit = 4
    blk = pl.BlockSpec((parts, unit, width, chan), lambda d, r: (d, first // unit + r, 0, 0))
    in_specs = [blk, pl.BlockSpec((parts, unit, width, chan), lambda d, r: (d, r, 0, 0)),
                pl.BlockSpec(w_o.shape, lambda d, r: (0, 0))]
    args = [z_parts, gated, w_o]
    alias = {}
    if prev is not None:
        in_specs.append(pl.BlockSpec(memory_space=pl.ANY))
        args.append(prev)
        alias = {3: 0}
    return pl.pallas_call(
        finish_kernel, name='finish_rows', grid=(n_col // parts, count // unit), in_specs=in_specs, out_specs=blk,
        out_shape=jax.ShapeDtypeStruct(z_parts.shape, z_parts.dtype),
        input_output_aliases=alias,
        cost_estimate=pl.CostEstimate(flops=n_col * count * width * chan * chan * 2 * 4, transcendentals=0,
                                      bytes_accessed=n_col * count * width * chan * 6),
        compiler_params=pltpu.CompilerParams(dimension_semantics=('arbitrary', 'arbitrary'), vmem_limit_bytes=VMEM_ALL),
    )(*args)


def solution(mesh):
    n_col, n_row = mesh.shape['col'], mesh.shape['row']
    tile_spec = P(('dp', 'row'), 'col', None)

    def per_device(pair_tile, res_mask, ln_gamma, ln_beta, w_q, w_k, w_v, w_b, w_g, w_o):
        row_len, width, chan = pair_tile.shape
        heads = w_b.shape[1]
        keys = n_col * width
        scale = (w_q.shape[1] // heads) ** -0.5
        rows = row_len // n_col
        w_rep = jnp.repeat(w_b.astype(jnp.float32), GROUP, axis=1)
        a_rows, ball = exchange(n_col, n_row, pair_tile, ln_gamma.reshape(1, chan), ln_beta.reshape(1, chan), w_rep, heads)
        mask = res_mask.reshape(1, keys)
        z_parts = pair_tile.reshape(n_col, rows, width, chan)
        home, first = [], 0
        for share in SHARES:
            count = rows * share // sum(SHARES)
            gated = attend(first, count, a_rows, ball, mask, (w_q, w_k, w_v, w_g), scale)
            home.append((first, count, lax.all_to_all(gated, 'col', 0, 0, tiled=True)))
            first += count
        out = None
        for first, count, gated in home:
            out = finish(first, count, z_parts, gated, w_o, out)
        return out.reshape(row_len, width, chan)

    return jax.shard_map(per_device, mesh=mesh, in_specs=(tile_spec, P('dp'), P(), P(), P(), P(), P(), P(), P(), P()), out_specs=tile_spec, check_vma=False)
```

profile of v0, /device:TPU:104, one launch (start us, length us, event | category | flops | bytes accessed | tf_op | source)
XLA Modules:
  0.0 201.3 jit_solution(3617088451059524582)
XLA Ops:
  0.0 1.3 reshape.23.mask_ref
  1.3 0.7 broadcast_in_dim.3
  2.0 0.7 copy.13.wrep_ref
  2.7 68.0 %exchange_rows.1 = (bf16[8,24,96,128]{3,2,1,0:T(8,128)(2,1)}, bf16[4,8,4,96,192]{4,3,2,1,0:T(8,128)(2,1)}) custom-call(bf16[8,24,96,128]{3,2,1,0:T(8,128)(2,1)} %bitcast.5, f32[1,128]{1,0:T(1,128)} %bitcast.9, f32[1,128]{1,0:T(1,128)} %bitcast.10, f32[128,128]{1,0:T(8,128)} %copy.13.wrep_ref), custom_call_target="tpu_custom_call" | custom-call | tf_op jit(solution)/shard_map/exchange_rows/pallas_call | solution.py:169
  70.7 57.3 %attend_rows.3 = bf16[8,16,96,128]{3,2,1,0:T(8,128)(2,1)} custom-call(bf16[8,24,96,128]{3,2,1,0:T(8,128)(2,1)} %get-tuple-element.7.a_ref, bf16[4,8,4,96,192]{4,3,2,1,0:T(8,128)(2,1)} %get-tuple-element.8.ball_ref, s32[1,768]{1,0:T(1,128)} %reshape.23.mask_ref, bf16[128,128]{1,0:T(8,128)(2,1)} %wq_ref.3, bf16[128,128]{1,0:T(8,128)(2,1)} %wk_ref.3, ...), custom_call_target="tpu_custom_call" | custom-call | flops 225485783040 | bytes 11010048 | tf_op jit(solution)/shard_map/attend_rows/pallas_call | solution.py:310
  128.0 4.8 %all-to-all-start.1 = ((bf16[8,16,96,128]{3,2,1,0:T(8,128)(2,1)}), bf16[8,16,96,128]{3,2,1,0:T(8,128)(2,1)}, u32[]{:S(2)}, u32[]{:S(2)}) async-start(bf16[8,16,96,128]{3,2,1,0:T(8,128)(2,1)} %attend_rows.3), calls=%async_computation.1 | async-start | bytes 6291456 | tf_op jit(solution)/shard_map/all_to_all | solution.py:371
  132.8 32.1 %attend_rows.2 = bf16[8,8,96,128]{3,2,1,0:T(8,128)(2,1)} custom-call(bf16[8,24,96,128]{3,2,1,0:T(8,128)(2,1)} %get-tuple-element.7.a_ref, bf16[4,8,4,96,192]{4,3,2,1,0:T(8,128)(2,1)} %get-tuple-element.8.ball_ref, s32[1,768]{1,0:T(1,128)} %reshape.23.mask_ref, bf16[128,128]{1,0:T(8,128)(2,1)} %wq_ref.3, bf16[128,128]{1,0:T(8,128)(2,1)} %wk_ref.3, ...), custom_call_target="tpu_custom_call" | custom-call | flops 112742891520 | bytes 7864320 | tf_op jit(solution)/shard_map/attend_rows/pallas_call | solution.py:310
  164.9 6.2 %all-to-all-done.1.g_ref = bf16[8,16,96,128]{3,2,1,0:T(8,128)(2,1)} async-done(((bf16[8,16,96,128]{3,2,1,0:T(8,128)(2,1)}), bf16[8,16,96,128]{3,2,1,0:T(8,128)(2,1)}, u32[]{:S(2)}, u32[]{:S(2)}) %all-to-all-start.1) | async-done | bytes 3145760 | tf_op jit(solution)/shard_map/all_to_all | solution.py:371
  171.1 4.5 %all-to-all-start = ((bf16[8,8,96,128]{3,2,1,0:T(8,128)(2,1)}), bf16[8,8,96,128]{3,2,1,0:T(8,128)(2,1)}, u32[]{:S(2)}, u32[]{:S(2)}) async-start(bf16[8,8,96,128]{3,2,1,0:T(8,128)(2,1)} %attend_rows.2), calls=%async_computation | async-start | bytes 3145728 | tf_op jit(solution)/shard_map/all_to_all | solution.py:371
  175.6 7.6 %finish_rows.2.rest_0_ = bf16[8,24,96,128]{3,2,1,0:T(8,128)(2,1)} custom-call(bf16[8,24,96,128]{3,2,1,0:T(8,128)(2,1)} %bitcast.6, bf16[8,16,96,128]{3,2,1,0:T(8,128)(2,1)} %all-to-all-done.1.g_ref, bf16[128,128]{1,0:T(8,128)(2,1)} %wo_ref.3), custom_call_target="tpu_custom_call" | custom-call | flops 1610612736 | bytes 9437184 | tf_op jit(solution)/shard_map/finish_rows/pallas_call | solution.py:343
  183.1 13.9 %all-to-all-done.g_ref = bf16[8,8,96,128]{3,2,1,0:T(8,128)(2,1)} async-done(((bf16[8,8,96,128]{3,2,1,0:T(8,128)(2,1)}), bf16[8,8,96,128]{3,2,1,0:T(8,128)(2,1)}, u32[]{:S(2)}, u32[]{:S(2)}) %all-to-all-start) | async-done | bytes 1572896 | tf_op jit(solution)/shard_map/all_to_all | solution.py:371
  197.0 4.3 %finish_rows.3 = bf16[8,24,96,128]{3,2,1,0:T(8,128)(2,1)} custom-call(bf16[8,24,96,128]{3,2,1,0:T(8,128)(2,1)} %bitcast.7, bf16[8,8,96,128]{3,2,1,0:T(8,128)(2,1)} %all-to-all-done.g_ref, bf16[128,128]{1,0:T(8,128)(2,1)} %wo_ref.3, bf16[8,24,96,128]{3,2,1,0:T(8,128)(2,1)} %finish_rows.2.rest_0_), custom_call_target="tpu_custom_call", output_to_operand_aliasing={{}: (3, {})} | custom-call | flops 805306368 | bytes 4718592 | tf_op jit(solution)/shard_map/finish_rows/pallas_call | solution.py:343
Async XLA Ops:
  128.0 43.1 %all-to-all-start.1 = ((bf16[8,16,96,128]{3,2,1,0:T(8,128)(2,1)}), bf16[8,16,96,128]{3,2,1,0:T(8,128)(2,1)}, u32[]{:S(2)}, u32[]{:S(2)}) async-start(bf16[8,16,96,128]{3,2,1,0:T(8,128)(2,1)} %attend_rows.3), calls=%async_computation.1 | async-start | bytes 6291456 | tf_op jit(solution)/shard_map/all_to_all | solution.py:371
  171.1 25.9 %all-to-all-start = ((bf16[8,8,96,128]{3,2,1,0:T(8,128)(2,1)}), bf16[8,8,96,128]{3,2,1,0:T(8,128)(2,1)}, u32[]{:S(2)}, u32[]{:S(2)}) async-start(bf16[8,8,96,128]{3,2,1,0:T(8,128)(2,1)} %attend_rows.2), calls=%async_computation | async-start | bytes 3145728 | tf_op jit(solution)/shard_map/all_to_all | solution.py:371
where the time goes:
time: 204 us; the launch traced here: 201 us
  Pallas kernels  169 us (83%)
  waiting for transfers between devices  20.1 us (10%)
  starting transfers between devices  9.3 us (5%)
  local copies, waits for them, and re-layouts  2.69 us (1%)
    pallas_call x2, Pallas kernels, attend(): pl.pallas_call(functools.partial(attend_kernel, scale), name='attend_rows...  89.4 us
    pallas_call x1, Pallas kernels, exchange(): pl.pallas_call(functools.partial(exchange_kernel, n_col, n_row), name='ex...  68 us
    all_to_all x2, waiting for transfers between devices, per_device(): home.append((first, count, lax.all_to_all(gated, 'col', 0, 0, tiled=True)))  20.1 us
    pallas_call x2, Pallas kernels, finish(): pl.pallas_call(finish_kernel, name='finish_rows', grid=(n_col // parts, c...  11.8 us
    all_to_all x2, starting transfers between devices, per_device(): home.append((first, count, lax.all_to_all(gated, 'col', 0, 0, tiled=True)))  9.3 us
  transfers between devices with their start and end apart: 2, of which 2 were waited for; matrix products, arithmetic and copies ran while one was open for 0% of the time, Pallas kernels for 20%

commit v1 on v0

--- a/solution.py
+++ b/solution.py
@@ -13,11 +13,11 @@
 SAFE = 1e-15
 MESH = pl.DeviceIdType.MESH
 GROUP = 32
-QTILE = 256
-KEYBLK = 128
-EARLY = 2
+QTILE = 768
+KEYBLK = 256
+EARLY = 4
 VMEM_ALL = 67043328
-PAIR = 2
+PAIR = 4
 UNROLL = 4
 SHARES = (2, 1)
 
@@ -31,7 +31,7 @@
     partner = me + 1 - 2 * lax.rem(me, 2)
 
     loads = []
-    order = [2, n_col - 2, n_col // 2]
+    order = [2, n_col - 2, 1, n_col - 1]
     order += [k for k in range(1, n_col) if k not in order] + [0]
     dests = [lax.rem(me + k, n_col) for k in order]
     for slot, dest in enumerate(dests):
@@ -49,7 +49,7 @@
     stat = jnp.full((2 * chan, chan), 1.0 / chan, jnp.bfloat16)
     gamma = gamma_ref[...]
     beta = beta_ref[...]
-    step_rows = rows // 2
+    step_rows = rows
 
     def norm_part(slot, dest):
         def body(step, carry):

time: 204 us -> 207 us (1.015)
  Pallas kernels: 169 us -> 159 us
  starting transfers between devices: 9.3 us -> 17.7 us
  waiting for transfers between devices: 20.1 us -> 23.4 us
    pallas_call x2, Pallas kernels: 89.4 us -> 79.9 us  [attend(): pl.pallas_call(functools.partial(attend_kernel, scale), name='attend_rows...]
    all_to_all x2, starting transfers between devices: 9.3 us -> 17.7 us  [per_device(): home.append((first, count, lax.all_to_all(gated, 'col', 0, 0, tiled=True)))]
    all_to_all x2, waiting for transfers between devices: 20.1 us -> 23.4 us  [per_device(): home.append((first, count, lax.all_to_all(gated, 'col', 0, 0, tiled=True)))]
  transfers between devices with their start and end apart: 2 -> 2, of which waited for: 2 -> 2; matrix products, arithmetic and copies ran while one was open for 0% -> 0% of each run, Pallas kernels for 20% -> 18%
where the time goes in v1:
time: 207 us; the launch traced here: 203 us
  Pallas kernels  159 us (77%)
  waiting for transfers between devices  23.4 us (11%)
  starting transfers between devices  17.7 us (9%)
  local copies, waits for them, and re-layouts  2.69 us (1%)
    pallas_call x2, Pallas kernels, attend(): pl.pallas_call(functools.partial(attend_kernel, scale), name='attend_rows...  79.9 us
    pallas_call x1, Pallas kernels, exchange(): pl.pallas_call(functools.partial(exchange_kernel, n_col, n_row), name='ex...  67.2 us
    all_to_all x2, waiting for transfers between devices, per_device(): home.append((first, count, lax.all_to_all(gated, 'col', 0, 0, tiled=True)))  23.4 us
    all_to_all x2, starting transfers between devices, per_device(): home.append((first, count, lax.all_to_all(gated, 'col', 0, 0, tiled=True)))  17.7 us
    pallas_call x2, Pallas kernels, finish(): pl.pallas_call(finish_kernel, name='finish_rows', grid=(n_col // parts, c...  11.8 us
  transfers between devices with their start and end apart: 2, of which 2 were waited for; matrix products, arithmetic and copies ran while one was open for 0% of the time, Pallas kernels for 18%

profile of v1, /device:TPU:104, one launch (start us, length us, event | category | flops | bytes accessed | tf_op | source)
XLA Modules:
  0.0 202.8 jit_solution(12327112086307629697)
XLA Ops:
  0.0 1.3 reshape.23.mask_ref
  1.3 0.7 broadcast_in_dim.3
  2.0 0.7 copy.13.wrep_ref
  2.7 67.2 %exchange_rows.1 = (bf16[8,24,96,128]{3,2,1,0:T(8,128)(2,1)}, bf16[4,8,4,96,192]{4,3,2,1,0:T(8,128)(2,1)}) custom-call(bf16[8,24,96,128]{3,2,1,0:T(8,128)(2,1)} %bitcast.5, f32[1,128]{1,0:T(1,128)} %bitcast.9, f32[1,128]{1,0:T(1,128)} %bitcast.10, f32[128,128]{1,0:T(8,128)} %copy.13.wrep_ref), custom_call_target="tpu_custom_call" | custom-call | tf_op jit(solution)/shard_map/exchange_rows/pallas_call | solution.py:169
  69.9 50.9 %attend_rows.3 = bf16[8,16,96,128]{3,2,1,0:T(8,128)(2,1)} custom-call(bf16[8,24,96,128]{3,2,1,0:T(8,128)(2,1)} %get-tuple-element.7.a_ref, bf16[4,8,4,96,192]{4,3,2,1,0:T(8,128)(2,1)} %get-tuple-element.8.ball_ref, s32[1,768]{1,0:T(1,128)} %reshape.23.mask_ref, bf16[128,128]{1,0:T(8,128)(2,1)} %wq_ref.3, bf16[128,128]{1,0:T(8,128)(2,1)} %wk_ref.3, ...), custom_call_target="tpu_custom_call" | custom-call | flops 225485783040 | bytes 11010048 | tf_op jit(solution)/shard_map/attend_rows/pallas_call | solution.py:310
  120.8 13.3 %all-to-all-start.1 = ((bf16[8,16,96,128]{3,2,1,0:T(8,128)(2,1)}), bf16[8,16,96,128]{3,2,1,0:T(8,128)(2,1)}, u32[]{:S(2)}, u32[]{:S(2)}) async-start(bf16[8,16,96,128]{3,2,1,0:T(8,128)(2,1)} %attend_rows.3), calls=%async_computation.1 | async-start | bytes 6291456 | tf_op jit(solution)/shard_map/all_to_all | solution.py:371
  134.1 29.0 %attend_rows.2 = bf16[8,8,96,128]{3,2,1,0:T(8,128)(2,1)} custom-call(bf16[8,24,96,128]{3,2,1,0:T(8,128)(2,1)} %get-tuple-element.7.a_ref, bf16[4,8,4,96,192]{4,3,2,1,0:T(8,128)(2,1)} %get-tuple-element.8.ball_ref, s32[1,768]{1,0:T(1,128)} %reshape.23.mask_ref, bf16[128,128]{1,0:T(8,128)(2,1)} %wq_ref.3, bf16[128,128]{1,0:T(8,128)(2,1)} %wk_ref.3, ...), custom_call_target="tpu_custom_call" | custom-call | flops 112742891520 | bytes 7864320 | tf_op jit(solution)/shard_map/attend_rows/pallas_call | solution.py:310
  163.0 9.5 %all-to-all-done.1.g_ref = bf16[8,16,96,128]{3,2,1,0:T(8,128)(2,1)} async-done(((bf16[8,16,96,128]{3,2,1,0:T(8,128)(2,1)}), bf16[8,16,96,128]{3,2,1,0:T(8,128)(2,1)}, u32[]{:S(2)}, u32[]{:S(2)}) %all-to-all-start.1) | async-done | bytes 3145760 | tf_op jit(solution)/shard_map/all_to_all | solution.py:371
  172.6 4.5 %all-to-all-start = ((bf16[8,8,96,128]{3,2,1,0:T(8,128)(2,1)}), bf16[8,8,96,128]{3,2,1,0:T(8,128)(2,1)}, u32[]{:S(2)}, u32[]{:S(2)}) async-start(bf16[8,8,96,128]{3,2,1,0:T(8,128)(2,1)} %attend_rows.2), calls=%async_computation | async-start | bytes 3145728 | tf_op jit(solution)/shard_map/all_to_all | solution.py:371
  177.1 7.6 %finish_rows.2.rest_0_ = bf16[8,24,96,128]{3,2,1,0:T(8,128)(2,1)} custom-call(bf16[8,24,96,128]{3,2,1,0:T(8,128)(2,1)} %bitcast.6, bf16[8,16,96,128]{3,2,1,0:T(8,128)(2,1)} %all-to-all-done.1.g_ref, bf16[128,128]{1,0:T(8,128)(2,1)} %wo_ref.3), custom_call_target="tpu_custom_call" | custom-call | flops 1610612736 | bytes 9437184 | tf_op jit(solution)/shard_map/finish_rows/pallas_call | solution.py:343
  184.6 13.9 %all-to-all-done.g_ref = bf16[8,8,96,128]{3,2,1,0:T(8,128)(2,1)} async-done(((bf16[8,8,96,128]{3,2,1,0:T(8,128)(2,1)}), bf16[8,8,96,128]{3,2,1,0:T(8,128)(2,1)}, u32[]{:S(2)}, u32[]{:S(2)}) %all-to-all-start) | async-done | bytes 1572896 | tf_op jit(solution)/shard_map/all_to_all | solution.py:371
  198.5 4.3 %finish_rows.3 = bf16[8,24,96,128]{3,2,1,0:T(8,128)(2,1)} custom-call(bf16[8,24,96,128]{3,2,1,0:T(8,128)(2,1)} %bitcast.7, bf16[8,8,96,128]{3,2,1,0:T(8,128)(2,1)} %all-to-all-done.g_ref, bf16[128,128]{1,0:T(8,128)(2,1)} %wo_ref.3, bf16[8,24,96,128]{3,2,1,0:T(8,128)(2,1)} %finish_rows.2.rest_0_), custom_call_target="tpu_custom_call", output_to_operand_aliasing={{}: (3, {})} | custom-call | flops 805306368 | bytes 4718592 | tf_op jit(solution)/shard_map/finish_rows/pallas_call | solution.py:343
Async XLA Ops:
  120.8 51.8 %all-to-all-start.1 = ((bf16[8,16,96,128]{3,2,1,0:T(8,128)(2,1)}), bf16[8,16,96,128]{3,2,1,0:T(8,128)(2,1)}, u32[]{:S(2)}, u32[]{:S(2)}) async-start(bf16[8,16,96,128]{3,2,1,0:T(8,128)(2,1)} %attend_rows.3), calls=%async_computation.1 | async-start | bytes 6291456 | tf_op jit(solution)/shard_map/all_to_all | solution.py:371
  172.6 25.9 %all-to-all-start = ((bf16[8,8,96,128]{3,2,1,0:T(8,128)(2,1)}), bf16[8,8,96,128]{3,2,1,0:T(8,128)(2,1)}, u32[]{:S(2)}, u32[]{:S(2)}) async-start(bf16[8,8,96,128]{3,2,1,0:T(8,128)(2,1)} %attend_rows.2), calls=%async_computation | async-start | bytes 3145728 | tf_op jit(solution)/shard_map/all_to_all | solution.py:371
